TPU v7x, 32 devices: a whole 2x2x4 slice. The times are simulated.
32 devices in a mesh: py: 4 (over y, core), pz: 8 (over z, x).
Axes of the slice: x: 2, y: 2, z: 4, core: 2. Of those that a mesh axis runs over, the one named last changes fastest.
Arguments:
- wavefunctions: float32 [2, 8, 128, 128, 128], P(None, None, 'pz', 'py'), may hold values from -6 to 6
- potential: float32 [128, 128, 128], P('pz', 'py'), may hold values from -4 to 4
- cutoff_sq: int32 [1], replicated, may hold values from 2304 to 4096
- locked_mask: int32 [8], replicated, may hold values 0 or 1
Outputs:
- applied: float32 [2, 8, 128, 128, 128], P(None, None, 'pz', 'py')
- rayleigh: float32 [8], replicated
- residual_norm: float32 [8], replicated
All inputs are finite; a program needn't handle non-finite values.
Results may differ from a plain program's by a relative error of at most 0.00005.
Values sent between devices are 32-bit elements; how exact they have to be, the bound alone decides.
A program may use at most 64 MiB of HBM per device.

v0:
```python
import math
import jax
import jax.numpy as jnp
from jax import lax
from jax.sharding import PartitionSpec as P


def make_tables(length, inverse):
    counter = jnp.arange(length, dtype=jnp.int32)
    phase = counter[:, None] * counter[None, :] % length
    angle = 2.0 * math.pi / length * phase.astype(jnp.float32)
    if inverse:
        return (jnp.cos(angle) / length, jnp.sin(angle) / length)
    return (jnp.cos(angle), -jnp.sin(angle))


def transform_axis(field, axis, tables):
    cosines, sines = tables
    letters = "abcdefgh"[: field.ndim - 1]
    place = axis - 1
    source = letters[:place] + "n" + letters[place + 1 :]
    target = letters[:place] + "k" + letters[place + 1 :]
    form = source + ",kn->" + target
    real_part = field[0]
    imag_part = field[1]
    high = lax.Precision.HIGHEST
    out_real = jnp.einsum(form, real_part, cosines, precision=high) - jnp.einsum(
        form, imag_part, sines, precision=high
    )
    out_imag = jnp.einsum(form, real_part, sines, precision=high) + jnp.einsum(
        form, imag_part, cosines, precision=high
    )
    return jnp.stack([out_real, out_imag])


def signed_square(counter, length):
    signed = jnp.where(counter < length // 2, counter, counter - length)
    return signed * signed


def kinetic_table(first_sq, second_sq, third_sq, cutoff_sq, length):
    total = first_sq[:, None, None] + second_sq[None, :, None] + third_sq[None, None, :]
    keep = (total <= cutoff_sq[0]).astype(jnp.float32)
    return 0.5 * (math.pi / length) ** 2 * total.astype(jnp.float32) * keep


def slab_kinetic(field, cutoff_sq, forward, inverse):
    parts, bands, rows_z, rows_y, length = field.shape
    size_y = lax.axis_size("py")
    size_z = lax.axis_size("pz")
    along_x = transform_axis(field, 4, forward)
    flat = jnp.moveaxis(along_x, 1, 3).reshape(parts, rows_z, rows_y, bands * length)
    planes = lax.all_to_all(
        lax.all_to_all(flat, "py", split_axis=3, concat_axis=2, tiled=True),
        "pz",
        split_axis=3,
        concat_axis=1,
        tiled=True,
    )
    width = planes.shape[3]
    start = lax.axis_index("py") * (bands * length // size_y) + lax.axis_index("pz") * width
    column = start + jnp.arange(width, dtype=jnp.int32)
    full_counter = jnp.arange(length, dtype=jnp.int32)
    full_sq = signed_square(full_counter, length)
    kinetic = kinetic_table(
        full_sq, full_sq, signed_square(column % length, length), cutoff_sq, length
    )
    spectrum = transform_axis(transform_axis(planes, 1, forward), 2, forward) * kinetic
    spatial = transform_axis(transform_axis(spectrum, 2, inverse), 1, inverse)
    returned = lax.all_to_all(
        lax.all_to_all(spatial, "py", split_axis=2, concat_axis=3, tiled=True),
        "pz",
        split_axis=1,
        concat_axis=3,
        tiled=True,
    )
    ordered = returned.reshape(parts, rows_z, rows_y, size_z, size_y, width)
    ordered = jnp.swapaxes(ordered, 3, 4).reshape(parts, rows_z, rows_y, bands, length)
    return transform_axis(jnp.moveaxis(ordered, 3, 1), 4, inverse)


def apply_kinetic(field, cutoff_sq, forward, inverse):
    return slab_kinetic(field, cutoff_sq, forward, inverse)


def body(wavefunctions, potential, cutoff_sq, locked_mask):
    length = wavefunctions.shape[4]
    forward = make_tables(length, False)
    inverse = make_tables(length, True)
    blocks = wavefunctions.shape[1] // 4

    def one_block(block, result):
        piece = lax.dynamic_slice_in_dim(wavefunctions, block * 4, 4, 1)
        done = apply_kinetic(piece, cutoff_sq, forward, inverse)
        return lax.dynamic_update_slice_in_dim(result, done, block * 4, 1)

    kinetic_part = lax.fori_loop(0, blocks, one_block, jnp.zeros_like(wavefunctions))
    applied = kinetic_part + potential[None, None] * wavefunctions
    norm_local = jnp.sum(wavefunctions * wavefunctions, axis=(0, 2, 3, 4))
    correlation_local = jnp.sum(wavefunctions * applied, axis=(0, 2, 3, 4))
    norm_sq, correlation = lax.psum((norm_local, correlation_local), ("py", "pz"))
    rayleigh = correlation / norm_sq
    residual = applied - rayleigh[None, :, None, None, None] * wavefunctions
    residual_sq = lax.psum(jnp.sum(residual * residual, axis=(0, 2, 3, 4)), ("py", "pz"))
    residual_norm = jnp.sqrt(residual_sq / norm_sq) * (1.0 - locked_mask.astype(jnp.float32))
    return (applied, rayleigh, residual_norm)


def solution(mesh):
    in_specs = (P(None, None, "pz", "py", None), P("pz", "py", None), P(), P())
    out_specs = (P(None, None, "pz", "py", None), P(), P())
    return jax.shard_map(body, mesh=mesh, in_specs=in_specs, out_specs=out_specs, check_vma=False)
```

profile of v0, /device:TPU:0, one launch (start us, length us, event | category | flops | bytes accessed | tf_op | source)
XLA Modules:
  0.0 693.6 jit_solution(16688748125790381216)
XLA Ops:
  3.2 599.9 %while.18 = (s32[]{:T(128)}, f32[2,8,16,32,128]{4,3,2,1,0:T(8,128)}, f32[2,8,16,32,128]{4,3,2,1,0:T(8,128)}, s32[1]{0:T(128)}, s32[]{:T(128)}, /*index=5*/s32[]{...) while((s32[]{:T(128)}, ...), condition=%wide.region_1.2_spmd.clone.clone, body=%wide.region_0.1_spmd.clone.clone.sunk | while | flops 9676570624 | bytes 232916592 | solution.py:97
  13.3 7.5 %copy.142 = f32[2,16,32,4,128]{2,1,0,4,3:T(8,128)} copy(f32[2,16,32,4,128]{4,2,1,3,0:T(8,128)S(1)} %maximum_bitcast_fusion.2) | data formatting | bytes 4194304 | tf_op jit(solution)/shard_map/while/body/eval_jaxpr/reshape | solution.py:52
  26.9 30.2 %all_to_all.204 = f32[4,1,131072]{2,1,0:T(1,128)} all-to-all(f32[4,1,131072]{2,1,0:T(1,128)S(1)} %reshape.143), channel_id=1, replica_groups=mesh['py'=4,'pz'=8] {'py'}, dimensions={0} | all-to-all | bytes 4194304 | tf_op jit(solution)/shard_map/while/body/eval_jaxpr/all_to_all | solution.py:54
  57.6 7.7 %reduce.4 = f32[4,131072]{1,0:T(4,128)S(1)} reduce(f32[4,1,131072]{2,1,0:T(1,128)} %all_to_all.204, f32[]{:T(128)} %broadcast.656), dimensions={1}, to_apply=%all_to_all.178.reduce_sub_computation | reduce | bytes 4194308 | tf_op jit(solution)/shard_map/while/body/eval_jaxpr/all_to_all | solution.py:54
  81.3 6.9 all-to-all-start.1
  89.3 46.3 %all-to-all-done.1 = f32[2,16,128,128]{2,1,0,3:T(8,128)S(1)} async-done(((f32[2,16,128,128]{2,1,0,3:T(8,128)}), f32[2,16,128,128]{2,1,0,3:T(8,128)S(1)}, u32[]{:S(2)}, u32[]{:S(2)}) %all-to-all-start.1) | async-done | bytes 2097184 | tf_op jit(solution)/shard_map/while/body/eval_jaxpr/all_to_all | solution.py:53
  170.9 28.1 %all_to_all.205 = f32[2,128,128,16]{1,3,0,2:T(8,128)S(1)} all-to-all(f32[2,128,128,16]{1,3,0,2:T(8,128)S(1)} %copy.151), channel_id=1, replica_groups=mesh['py'=4,'pz'=8] {'py'}, dimensions={2} | all-to-all | bytes 4194304 | tf_op jit(solution)/shard_map/while/body/eval_jaxpr/all_to_all | solution.py:71
  203.8 7.2 %reshape.145 = f32[8,1,65536]{2,1,0:T(1,128)} reshape(f32[128,2,32,64]{3,2,1,0:T(8,128)} %bitcast.327) | data formatting | bytes 4194304 | tf_op jit(solution)/shard_map/while
  214.9 48.0 %all-to-all-done.3 = f32[8,1,65536]{2,1,0:T(1,128)S(1)} async-done(((f32[8,1,65536]{2,1,0:T(1,128)}), f32[8,1,65536]{2,1,0:T(1,128)S(1)}, u32[]{:S(2)}, u32[]{:S(2)}) %all-to-all-start.3) | async-done | bytes 2097184 | tf_op jit(solution)/shard_map/while/body/eval_jaxpr/all_to_all | solution.py:70
  264.8 7.2 %reduce.5 = f32[8,65536]{1,0:T(8,128)S(1)} reduce(f32[8,1,65536]{2,1,0:T(1,128)} %copy-done, f32[]{:T(128)} %broadcast.657), dimensions={1}, to_apply=%all_to_all.189.reduce_sub_computation | reduce | bytes 4194308 | tf_op jit(solution)/shard_map/while/body/eval_jaxpr/all_to_all | solution.py:70
  275.6 7.0 %copy.154 = f32[2,16,32,8,64]{2,4,3,1,0:T(8,128)} copy(f32[2,16,32,8,64]{4,2,0,1,3:T(8,128)} %bitcast.326) | data formatting | bytes 4194304 | tf_op jit(solution)/shard_map/while/body/eval_jaxpr/all_to_all | solution.py:70
  282.6 7.9 %copy.155 = f32[2,16,32,4,8,16]{2,5,4,3,1,0:T(8,128)} copy(f32[2,16,32,4,8,16]{2,5,3,4,1,0:T(8,128)} %bitcast.320) | data formatting | bytes 4194304 | tf_op jit(solution)/shard_map/while/body/eval_jaxpr/transpose | solution.py:78
  313.5 7.5 %copy.142 = f32[2,16,32,4,128]{2,1,0,4,3:T(8,128)} copy(f32[2,16,32,4,128]{4,2,1,3,0:T(8,128)S(1)} %maximum_bitcast_fusion.2) | data formatting | bytes 4194304 | tf_op jit(solution)/shard_map/while/body/eval_jaxpr/reshape | solution.py:52
  327.2 29.1 %all_to_all.204 = f32[4,1,131072]{2,1,0:T(1,128)} all-to-all(f32[4,1,131072]{2,1,0:T(1,128)S(1)} %reshape.143), channel_id=1, replica_groups=mesh['py'=4,'pz'=8] {'py'}, dimensions={0} | all-to-all | bytes 4194304 | tf_op jit(solution)/shard_map/while/body/eval_jaxpr/all_to_all | solution.py:54
  356.8 7.7 %reduce.4 = f32[4,131072]{1,0:T(4,128)S(1)} reduce(f32[4,1,131072]{2,1,0:T(1,128)} %all_to_all.204, f32[]{:T(128)} %broadcast.656), dimensions={1}, to_apply=%all_to_all.178.reduce_sub_computation | reduce | bytes 4194308 | tf_op jit(solution)/shard_map/while/body/eval_jaxpr/all_to_all | solution.py:54
  385.6 46.7 %all-to-all-done.1 = f32[2,16,128,128]{2,1,0,3:T(8,128)S(1)} async-done(((f32[2,16,128,128]{2,1,0,3:T(8,128)}), f32[2,16,128,128]{2,1,0,3:T(8,128)S(1)}, u32[]{:S(2)}, u32[]{:S(2)}) %all-to-all-start.1) | async-done | bytes 2097184 | tf_op jit(solution)/shard_map/while/body/eval_jaxpr/all_to_all | solution.py:53
  467.6 28.1 %all_to_all.205 = f32[2,128,128,16]{1,3,0,2:T(8,128)S(1)} all-to-all(f32[2,128,128,16]{1,3,0,2:T(8,128)S(1)} %copy.151), channel_id=1, replica_groups=mesh['py'=4,'pz'=8] {'py'}, dimensions={2} | all-to-all | bytes 4194304 | tf_op jit(solution)/shard_map/while/body/eval_jaxpr/all_to_all | solution.py:71
  500.5 7.2 %reshape.145 = f32[8,1,65536]{2,1,0:T(1,128)} reshape(f32[128,2,32,64]{3,2,1,0:T(8,128)} %bitcast.327) | data formatting | bytes 4194304 | tf_op jit(solution)/shard_map/while
  511.6 48.0 %all-to-all-done.3 = f32[8,1,65536]{2,1,0:T(1,128)S(1)} async-done(((f32[8,1,65536]{2,1,0:T(1,128)}), f32[8,1,65536]{2,1,0:T(1,128)S(1)}, u32[]{:S(2)}, u32[]{:S(2)}) %all-to-all-start.3) | async-done | bytes 2097184 | tf_op jit(solution)/shard_map/while/body/eval_jaxpr/all_to_all | solution.py:70
  561.5 7.2 %reduce.5 = f32[8,65536]{1,0:T(8,128)S(1)} reduce(f32[8,1,65536]{2,1,0:T(1,128)} %copy-done, f32[]{:T(128)} %broadcast.657), dimensions={1}, to_apply=%all_to_all.189.reduce_sub_computation | reduce | bytes 4194308 | tf_op jit(solution)/shard_map/while/body/eval_jaxpr/all_to_all | solution.py:70
  572.3 7.0 %copy.154 = f32[2,16,32,8,64]{2,4,3,1,0:T(8,128)} copy(f32[2,16,32,8,64]{4,2,0,1,3:T(8,128)} %bitcast.326) | data formatting | bytes 4194304 | tf_op jit(solution)/shard_map/while/body/eval_jaxpr/all_to_all | solution.py:70
  579.3 7.9 %copy.155 = f32[2,16,32,4,8,16]{2,5,4,3,1,0:T(8,128)} copy(f32[2,16,32,4,8,16]{2,5,3,4,1,0:T(8,128)} %bitcast.320) | data formatting | bytes 4194304 | tf_op jit(solution)/shard_map/while/body/eval_jaxpr/transpose | solution.py:78
  609.6 37.5 %all-reduce = (f32[8]{0:T(128)S(1)}, f32[8]{0:T(128)S(1)}) all-reduce(f32[8]{0:T(128)S(1)} %get-tuple-element.349, f32[8]{0:T(128)S(1)} %get-tuple-element.348), channel_id=1, replica_groups=mesh['py'=4,'pz'=8] {'py','pz'}, use_global_device_ids=true, to_apply=%region_3.4 | all-reduce | flops 16 | bytes 128 | tf_op jit(solution)/shard_map/psum | solution.py:101
  651.4 41.5 %psum.23 = f32[8]{0:T(128)S(1)} all-reduce(f32[8]{0:T(128)S(1)} %multiply_reduce_fusion), channel_id=1, replica_groups=mesh['py'=4,'pz'=8] {'py','pz'}, use_global_device_ids=true, to_apply=%region_7.8 | all-reduce | flops 8 | bytes 64 | tf_op jit(solution)/shard_map/psum | solution.py:104
  (130 shorter events, 209.5 us)
Async XLA Ops:
  3.2 599.9 %copy-start.4 = (f32[16,32,128]{2,1,0:T(8,128)S(1)}, f32[16,32,128]{2,1,0:T(8,128)}, u32[]{:S(2)}) copy-start(f32[16,32,128]{2,1,0:T(8,128)} %param.7) | copy-start | bytes 786436
  81.3 54.2 %all-to-all-start.1 = ((f32[2,16,128,128]{2,1,0,3:T(8,128)}), f32[2,16,128,128]{2,1,0,3:T(8,128)S(1)}, u32[]{:S(2)}, u32[]{:S(2)}) async-start(f32[2,16,128,128]{2,1,0,3:T(8,128)} %copy.145), calls=%async_computation.1 | async-start | bytes 4194304 | tf_op jit(solution)/shard_map/while/body/eval_jaxpr/all_to_all | solution.py:53
  138.5 3.5 copy-start.1
  211.0 51.9 %all-to-all-start.3 = ((f32[8,1,65536]{2,1,0:T(1,128)}), f32[8,1,65536]{2,1,0:T(1,128)S(1)}, u32[]{:S(2)}, u32[]{:S(2)}) async-start(f32[8,1,65536]{2,1,0:T(1,128)} %reshape.145), calls=%async_computation.3 | async-start | bytes 4194304 | tf_op jit(solution)/shard_map/while/body/eval_jaxpr/all_to_all | solution.py:70
  262.9 1.4 copy-start
  298.6 2.5 copy-start.2
  301.3 2.0 copy-start.3
  380.5 51.7 %all-to-all-start.1 = ((f32[2,16,128,128]{2,1,0,3:T(8,128)}), f32[2,16,128,128]{2,1,0,3:T(8,128)S(1)}, u32[]{:S(2)}, u32[]{:S(2)}) async-start(f32[2,16,128,128]{2,1,0,3:T(8,128)} %copy.145), calls=%async_computation.1 | async-start | bytes 4194304 | tf_op jit(solution)/shard_map/while/body/eval_jaxpr/all_to_all | solution.py:53
  435.2 3.5 copy-start.1
  507.7 51.9 %all-to-all-start.3 = ((f32[8,1,65536]{2,1,0:T(1,128)}), f32[8,1,65536]{2,1,0:T(1,128)S(1)}, u32[]{:S(2)}, u32[]{:S(2)}) async-start(f32[8,1,65536]{2,1,0:T(1,128)} %reshape.145), calls=%async_computation.3 | async-start | bytes 4194304 | tf_op jit(solution)/shard_map/while/body/eval_jaxpr/all_to_all | solution.py:70
  559.6 1.4 copy-start
  595.2 2.5 copy-start.2
  598.0 2.0 copy-start.3
  647.1 4.2 copy-start.5
  647.2 45.7 %copy-start.6 = (s32[8]{0:T(128)S(1)}, s32[8]{0:T(128)}, u32[]{:S(2)}) copy-start(s32[8]{0:T(128)} %param.9) | copy-start | bytes 100
where the time goes:
time: 697 us; the launch traced here: 694 us
  blocking collectives  195 us (28%)
  waiting for transfers between devices  189 us (27%)
  local copies, waits for them, and re-layouts  156 us (22%)
  matrix products  85.4 us (12%)
  other arithmetic  44.8 us (6%)
  starting transfers between devices  18.7 us (3%)
    all_to_all x2, waiting for transfers between devices, slab_kinetic(): lax.all_to_all(lax.all_to_all(spatial, 'py', split_axis=2, concat_axis=3,...  96 us
    all_to_all x2, waiting for transfers between devices, slab_kinetic(): lax.all_to_all(lax.all_to_all(flat, 'py', split_axis=3, concat_axis=2, ti...  92.9 us
    all_to_all x2, blocking collectives, slab_kinetic(): lax.all_to_all(flat, 'py', split_axis=3, concat_axis=2, tiled=True)  59.3 us
    all_to_all x2, blocking collectives, slab_kinetic(): lax.all_to_all(spatial, 'py', split_axis=2, concat_axis=3, tiled=True)  56.3 us
    while x24, local copies, waits for them, and re-layouts  52.9 us
    psum x1, blocking collectives, body(): lax.psum(jnp.sum(residual * residual, axis=(0, 2, 3, 4)), ('py', 'pz'))  41.5 us
    psum x1, blocking collectives, body(): lax.psum((norm_local, correlation_local), ('py', 'pz'))  37.5 us
    dot_general x12, matrix products, transform_axis(): jnp.einsum(form, imag_part, sines, precision=high)  22.5 us
  transfers between devices with their start and end apart: 4, of which 4 were waited for; matrix products, arithmetic and copies ran while one was open for 0% of the time, Pallas kernels for 0%

commit v1 on v0

--- a/solution.py
+++ b/solution.py
@@ -3,6 +3,13 @@
 import jax.numpy as jnp
 from jax import lax
 from jax.sharding import PartitionSpec as P
+
+
+def exchange_blocks(array, mesh_axis, split, join):
+    devices = lax.axis_size(mesh_axis)
+    pieces = jnp.stack(jnp.split(array, devices, axis=split), axis=0)
+    pieces = lax.all_to_all(pieces, mesh_axis, split_axis=0, concat_axis=0)
+    return jnp.concatenate(pieces, axis=join)
 
 
 def make_tables(length, inverse):
@@ -68,11 +75,7 @@
     spectrum = transform_axis(transform_axis(planes, 1, forward), 2, forward) * kinetic
     spatial = transform_axis(transform_axis(spectrum, 2, inverse), 1, inverse)
     returned = lax.all_to_all(
-        lax.all_to_all(spatial, "py", split_axis=2, concat_axis=3, tiled=True),
-        "pz",
-        split_axis=1,
-        concat_axis=3,
-        tiled=True,
+        exchange_blocks(spatial, "py", 2, 3), "pz", split_axis=1, concat_axis=3, tiled=True
     )
     ordered = returned.reshape(parts, rows_z, rows_y, size_z, size_y, width)
     ordered = jnp.swapaxes(ordered, 3, 4).reshape(parts, rows_z, rows_y, bands, length)

time: 697 us -> 697 us (level)
    reshape x0 -> x4, local copies, waits for them, and re-layouts: none -> 11.4 us  [exchange_blocks(): return jnp.concatenate(pieces, axis=join)]
    all_to_all x8 -> x4, local copies, waits for them, and re-layouts: 24.5 us -> 15 us  [slab_kinetic(): lax.all_to_all(exchange_blocks(spatial, 'py', 2, 3), 'pz', split_axis=1,...]
where the time goes in v1:
time: 697 us; the launch traced here: 694 us
  blocking collectives  195 us (28%)
  waiting for transfers between devices  189 us (27%)
  local copies, waits for them, and re-layouts  156 us (22%)
  matrix products  85.3 us (12%)
  other arithmetic  45.2 us (6%)
  starting transfers between devices  18.7 us (3%)
    all_to_all x2, waiting for transfers between devices, slab_kinetic(): lax.all_to_all(exchange_blocks(spatial, 'py', 2, 3), 'pz', split_axis=1,...  96 us
    all_to_all x2, waiting for transfers between devices, slab_kinetic(): lax.all_to_all(lax.all_to_all(flat, 'py', split_axis=3, concat_axis=2, ti...  92.9 us
    all_to_all x2, blocking collectives, slab_kinetic(): lax.all_to_all(flat, 'py', split_axis=3, concat_axis=2, tiled=True)  59.3 us
    all_to_all x2, blocking collectives, exchange_blocks(): pieces = lax.all_to_all(pieces, mesh_axis, split_axis=0, concat_axis=0)  56.3 us
    while x24, local copies, waits for them, and re-layouts  52.9 us
    psum x1, blocking collectives, body(): lax.psum(jnp.sum(residual * residual, axis=(0, 2, 3, 4)), ('py', 'pz'))  41.5 us
    psum x1, blocking collectives, body(): lax.psum((norm_local, correlation_local), ('py', 'pz'))  37.5 us
    dot_general x12, matrix products, transform_axis(): jnp.einsum(form, imag_part, sines, precision=high)  22.5 us
  transfers between devices with their start and end apart: 4, of which 4 were waited for; matrix products, arithmetic and copies ran while one was open for 0% of the time, Pallas kernels for 0%

profile of v1, /device:TPU:0, one launch (start us, length us, event | category | flops | bytes accessed | tf_op | source)
XLA Modules:
  0.0 693.5 jit_solution(15916022973731821663)
XLA Ops:
  3.2 599.8 %while.18 = (s32[]{:T(128)}, f32[2,8,16,32,128]{4,3,2,1,0:T(8,128)}, f32[2,8,16,32,128]{4,3,2,1,0:T(8,128)}, s32[1]{0:T(128)}, s32[]{:T(128)}, /*index=5*/s32[]{...) while((s32[]{:T(128)}, ...), condition=%wide.region_1.2_spmd.clone.clone, body=%wide.region_0.1_spmd.clone.clone.sunk | while | flops 9678143488 | bytes 232916592 | solution.py:100
  13.3 7.5 %copy.138 = f32[2,16,32,4,128]{2,1,0,4,3:T(8,128)} copy(f32[2,16,32,4,128]{4,2,1,3,0:T(8,128)S(1)} %maximum_bitcast_fusion.2) | data formatting | bytes 4194304 | tf_op jit(solution)/shard_map/while/body/eval_jaxpr/reshape | solution.py:59
  26.9 30.2 %all_to_all.164 = f32[4,1,131072]{2,1,0:T(1,128)} all-to-all(f32[4,1,131072]{2,1,0:T(1,128)S(1)} %reshape.169), channel_id=1, replica_groups=mesh['py'=4,'pz'=8] {'py'}, dimensions={0} | all-to-all | bytes 4194304 | tf_op jit(solution)/shard_map/while/body/eval_jaxpr/all_to_all | solution.py:61
  57.6 7.7 %reduce.4 = f32[4,131072]{1,0:T(4,128)S(1)} reduce(f32[4,1,131072]{2,1,0:T(1,128)} %all_to_all.164, f32[]{:T(128)} %broadcast.656), dimensions={1}, to_apply=%all_to_all.141.reduce_sub_computation | reduce | bytes 4194308 | tf_op jit(solution)/shard_map/while/body/eval_jaxpr/all_to_all | solution.py:61
  81.3 6.9 all-to-all-start.1
  89.3 46.3 %all-to-all-done.1 = f32[2,16,128,128]{2,1,0,3:T(8,128)S(1)} async-done(((f32[2,16,128,128]{2,1,0,3:T(8,128)}), f32[2,16,128,128]{2,1,0,3:T(8,128)S(1)}, u32[]{:S(2)}, u32[]{:S(2)}) %all-to-all-start.1) | async-done | bytes 2097184 | tf_op jit(solution)/shard_map/while/body/eval_jaxpr/all_to_all | solution.py:60
  169.9 28.1 %all_to_all.165 = f32[4,2,128,32,16]{2,3,4,1,0:T(8,128)S(1)} all-to-all(f32[4,2,128,32,16]{2,3,4,1,0:T(8,128)S(1)} %pad_maximum_fusion.3), channel_id=1, replica_groups=mesh['py'=4,'pz'=8] {'py'}, dimensions={0} | all-to-all | bytes 4194304 | tf_op jit(solution)/shard_map/while/body/eval_jaxpr/all_to_all | solution.py:11
  203.8 7.2 %reshape.171 = f32[8,1,65536]{2,1,0:T(1,128)} reshape(f32[128,2,32,64]{3,2,1,0:T(8,128)} %bitcast.335) | data formatting | bytes 4194304 | tf_op jit(solution)/shard_map/while
  214.9 48.0 %all-to-all-done.3 = f32[8,1,65536]{2,1,0:T(1,128)S(1)} async-done(((f32[8,1,65536]{2,1,0:T(1,128)}), f32[8,1,65536]{2,1,0:T(1,128)S(1)}, u32[]{:S(2)}, u32[]{:S(2)}) %all-to-all-start.3) | async-done | bytes 2097184 | tf_op jit(solution)/shard_map/while/body/eval_jaxpr/all_to_all | solution.py:77
  264.7 7.2 %reduce.5 = f32[8,65536]{1,0:T(8,128)S(1)} reduce(f32[8,1,65536]{2,1,0:T(1,128)} %copy-done, f32[]{:T(128)} %broadcast.657), dimensions={1}, to_apply=%all_to_all.149.reduce_sub_computation | reduce | bytes 4194308 | tf_op jit(solution)/shard_map/while/body/eval_jaxpr/all_to_all | solution.py:77
  275.6 7.0 %copy.149 = f32[2,16,32,8,64]{2,4,3,1,0:T(8,128)} copy(f32[2,16,32,8,64]{4,2,0,1,3:T(8,128)} %bitcast.334) | data formatting | bytes 4194304 | tf_op jit(solution)/shard_map/while/body/eval_jaxpr/all_to_all | solution.py:77
  282.6 7.9 %copy.150 = f32[2,16,32,4,8,16]{2,5,4,3,1,0:T(8,128)} copy(f32[2,16,32,4,8,16]{2,5,3,4,1,0:T(8,128)} %bitcast.328) | data formatting | bytes 4194304 | tf_op jit(solution)/shard_map/while/body/eval_jaxpr/transpose | solution.py:81
  313.5 7.5 %copy.138 = f32[2,16,32,4,128]{2,1,0,4,3:T(8,128)} copy(f32[2,16,32,4,128]{4,2,1,3,0:T(8,128)S(1)} %maximum_bitcast_fusion.2) | data formatting | bytes 4194304 | tf_op jit(solution)/shard_map/while/body/eval_jaxpr/reshape | solution.py:59
  327.1 29.1 %all_to_all.164 = f32[4,1,131072]{2,1,0:T(1,128)} all-to-all(f32[4,1,131072]{2,1,0:T(1,128)S(1)} %reshape.169), channel_id=1, replica_groups=mesh['py'=4,'pz'=8] {'py'}, dimensions={0} | all-to-all | bytes 4194304 | tf_op jit(solution)/shard_map/while/body/eval_jaxpr/all_to_all | solution.py:61
  356.7 7.7 %reduce.4 = f32[4,131072]{1,0:T(4,128)S(1)} reduce(f32[4,1,131072]{2,1,0:T(1,128)} %all_to_all.164, f32[]{:T(128)} %broadcast.656), dimensions={1}, to_apply=%all_to_all.141.reduce_sub_computation | reduce | bytes 4194308 | tf_op jit(solution)/shard_map/while/body/eval_jaxpr/all_to_all | solution.py:61
  385.5 46.7 %all-to-all-done.1 = f32[2,16,128,128]{2,1,0,3:T(8,128)S(1)} async-done(((f32[2,16,128,128]{2,1,0,3:T(8,128)}), f32[2,16,128,128]{2,1,0,3:T(8,128)S(1)}, u32[]{:S(2)}, u32[]{:S(2)}) %all-to-all-start.1) | async-done | bytes 2097184 | tf_op jit(solution)/shard_map/while/body/eval_jaxpr/all_to_all | solution.py:60
  466.5 28.1 %all_to_all.165 = f32[4,2,128,32,16]{2,3,4,1,0:T(8,128)S(1)} all-to-all(f32[4,2,128,32,16]{2,3,4,1,0:T(8,128)S(1)} %pad_maximum_fusion.3), channel_id=1, replica_groups=mesh['py'=4,'pz'=8] {'py'}, dimensions={0} | all-to-all | bytes 4194304 | tf_op jit(solution)/shard_map/while/body/eval_jaxpr/all_to_all | solution.py:11
  500.4 7.2 %reshape.171 = f32[8,1,65536]{2,1,0:T(1,128)} reshape(f32[128,2,32,64]{3,2,1,0:T(8,128)} %bitcast.335) | data formatting | bytes 4194304 | tf_op jit(solution)/shard_map/while
  511.5 48.0 %all-to-all-done.3 = f32[8,1,65536]{2,1,0:T(1,128)S(1)} async-done(((f32[8,1,65536]{2,1,0:T(1,128)}), f32[8,1,65536]{2,1,0:T(1,128)S(1)}, u32[]{:S(2)}, u32[]{:S(2)}) %all-to-all-start.3) | async-done | bytes 2097184 | tf_op jit(solution)/shard_map/while/body/eval_jaxpr/all_to_all | solution.py:77
  561.3 7.2 %reduce.5 = f32[8,65536]{1,0:T(8,128)S(1)} reduce(f32[8,1,65536]{2,1,0:T(1,128)} %copy-done, f32[]{:T(128)} %broadcast.657), dimensions={1}, to_apply=%all_to_all.149.reduce_sub_computation | reduce | bytes 4194308 | tf_op jit(solution)/shard_map/while/body/eval_jaxpr/all_to_all | solution.py:77
  572.2 7.0 %copy.149 = f32[2,16,32,8,64]{2,4,3,1,0:T(8,128)} copy(f32[2,16,32,8,64]{4,2,0,1,3:T(8,128)} %bitcast.334) | data formatting | bytes 4194304 | tf_op jit(solution)/shard_map/while/body/eval_jaxpr/all_to_all | solution.py:77
  579.2 7.9 %copy.150 = f32[2,16,32,4,8,16]{2,5,4,3,1,0:T(8,128)} copy(f32[2,16,32,4,8,16]{2,5,3,4,1,0:T(8,128)} %bitcast.328) | data formatting | bytes 4194304 | tf_op jit(solution)/shard_map/while/body/eval_jaxpr/transpose | solution.py:81
  609.5 37.5 %all-reduce = (f32[8]{0:T(128)S(1)}, f32[8]{0:T(128)S(1)}) all-reduce(f32[8]{0:T(128)S(1)} %get-tuple-element.349, f32[8]{0:T(128)S(1)} %get-tuple-element.348), channel_id=1, replica_groups=mesh['py'=4,'pz'=8] {'py','pz'}, use_global_device_ids=true, to_apply=%region_3.4 | all-reduce | flops 16 | bytes 128 | tf_op jit(solution)/shard_map/psum | solution.py:104
  651.3 41.5 %psum.23 = f32[8]{0:T(128)S(1)} all-reduce(f32[8]{0:T(128)S(1)} %multiply_reduce_fusion), channel_id=1, replica_groups=mesh['py'=4,'pz'=8] {'py','pz'}, use_global_device_ids=true, to_apply=%region_7.8 | all-reduce | flops 8 | bytes 64 | tf_op jit(solution)/shard_map/psum | solution.py:107
  (130 shorter events, 209.4 us)
Async XLA Ops:
  3.2 599.8 %copy-start.4 = (f32[16,32,128]{2,1,0:T(8,128)S(1)}, f32[16,32,128]{2,1,0:T(8,128)}, u32[]{:S(2)}) copy-start(f32[16,32,128]{2,1,0:T(8,128)} %param.7) | copy-start | bytes 786436
  81.3 54.2 %all-to-all-start.1 = ((f32[2,16,128,128]{2,1,0,3:T(8,128)}), f32[2,16,128,128]{2,1,0,3:T(8,128)S(1)}, u32[]{:S(2)}, u32[]{:S(2)}) async-start(f32[2,16,128,128]{2,1,0,3:T(8,128)} %copy.141), calls=%async_computation.1 | async-start | bytes 4194304 | tf_op jit(solution)/shard_map/while/body/eval_jaxpr/all_to_all | solution.py:60
  138.5 3.5 copy-start.1
  210.9 51.9 %all-to-all-start.3 = ((f32[8,1,65536]{2,1,0:T(1,128)}), f32[8,1,65536]{2,1,0:T(1,128)S(1)}, u32[]{:S(2)}, u32[]{:S(2)}) async-start(f32[8,1,65536]{2,1,0:T(1,128)} %reshape.171), calls=%async_computation.3 | async-start | bytes 4194304 | tf_op jit(solution)/shard_map/while/body/eval_jaxpr/all_to_all | solution.py:77
  262.9 1.4 copy-start
  298.5 2.5 copy-start.2
  301.3 2.0 copy-start.3
  380.5 51.7 %all-to-all-start.1 = ((f32[2,16,128,128]{2,1,0,3:T(8,128)}), f32[2,16,128,128]{2,1,0,3:T(8,128)S(1)}, u32[]{:S(2)}, u32[]{:S(2)}) async-start(f32[2,16,128,128]{2,1,0,3:T(8,128)} %copy.141), calls=%async_computation.1 | async-start | bytes 4194304 | tf_op jit(solution)/shard_map/while/body/eval_jaxpr/all_to_all | solution.py:60
  435.1 3.5 copy-start.1
  507.6 51.9 %all-to-all-start.3 = ((f32[8,1,65536]{2,1,0:T(1,128)}), f32[8,1,65536]{2,1,0:T(1,128)S(1)}, u32[]{:S(2)}, u32[]{:S(2)}) async-start(f32[8,1,65536]{2,1,0:T(1,128)} %reshape.171), calls=%async_computation.3 | async-start | bytes 4194304 | tf_op jit(solution)/shard_map/while/body/eval_jaxpr/all_to_all | solution.py:77
  559.5 1.4 copy-start
  595.1 2.5 copy-start.2
  597.9 2.0 copy-start.3
  647.0 4.2 copy-start.5
  647.0 45.7 %copy-start.6 = (s32[8]{0:T(128)S(1)}, s32[8]{0:T(128)}, u32[]{:S(2)}) copy-start(s32[8]{0:T(128)} %param.9) | copy-start | bytes 100
